TPU v7x, 32 devices: a whole 2x2x4 slice. The times are simulated.
32 devices in a mesh: section: 4 (over y, x), tensor: 2 (over core), dp: 4 (over z).
Axes of the slice: x: 2, y: 2, z: 4, core: 2. Of those that a mesh axis runs over, the one named last changes fastest.
Arguments:
- hidden_in: bfloat16 [128, 4096], P('dp', 'tensor'), may hold values from -6 to 6
- norm_gain: float32 [4, 4096], P('section'), may hold values from 0.25 to 1.75
- gate_weight: bfloat16 [4, 4096, 8192], P('section', 'dp', 'tensor'), may hold values from -0.09375 to 0.09375
- up_weight: bfloat16 [4, 4096, 8192], P('section', 'dp', 'tensor'), may hold values from -0.09375 to 0.09375
- down_weight: bfloat16 [4, 4096, 8192], P('section', 'dp', 'tensor'), may hold values from -0.0625 to 0.0625
- lengths: int32 [16], P('dp'), may hold values from 3 to 8
Outputs:
- rdm: float32 [4, 16, 16], P('section', 'dp')
Inputs may be any that keep to these rules, and one draw needn't show every extreme that they name: `lengths`: the number of leading valid token rows of each sentence.
All inputs are finite; a program needn't handle non-finite values.
Results may differ from a plain program's by a relative error of at most 0.0012.
Values may be sent and summed in bfloat16 or wider, within the bound.
A program may use at most 192 MiB of HBM per device.

v0:
```python
import jax
import jax.numpy as jnp
from jax import lax
from jax.sharding import PartitionSpec as P

RMS_EPS = 1e-05
UNIT_FLOOR = 0.1
CONTRACT_LAST = (((1,), (1,)), ((), ()))


def per_device(hidden_in, norm_gain, gate_weight, up_weight, down_weight, lengths):
    section = lax.axis_index("section")
    dp = lax.axis_index("dp")
    sections = lax.axis_size("section")
    dps = lax.axis_size("dp")
    gate, up, down = (gate_weight[0], up_weight[0], down_weight[0])
    width = gate.shape[0]
    d_model = width * dps
    gain = lax.dynamic_slice_in_dim(norm_gain[0], dp * width, width, 0)
    source = lax.all_gather(hidden_in, "tensor", axis=1, tiled=True)
    state = lax.all_to_all(source, "dp", split_axis=1, concat_axis=0, tiled=True)
    lens = lax.all_gather(lengths, "dp", axis=0, tiled=True)
    final = state
    pairs = [(i, i + 1) for i in range(sections - 1)]
    for tick in range(sections):
        wide = state.astype(jnp.float32)
        total = lax.psum(jnp.sum(wide * wide, axis=1, keepdims=True), "dp")
        normed = (wide * lax.rsqrt(total / d_model + RMS_EPS) * gain[None, :]).astype(jnp.bfloat16)
        g = jnp.dot(normed, gate, preferred_element_type=jnp.float32).astype(jnp.bfloat16)
        u = jnp.dot(normed, up, preferred_element_type=jnp.float32).astype(jnp.bfloat16)
        both = lax.psum_scatter(
            jnp.concatenate([g, u], axis=1), "dp", scatter_dimension=0, tiled=True
        )
        both = both.astype(jnp.float32)
        cols = gate.shape[1]
        hidden = (jax.nn.silu(both[:, :cols]) * both[:, cols:]).astype(jnp.bfloat16)
        hidden = lax.all_gather(hidden, "dp", axis=0, tiled=True)
        part = lax.dot_general(hidden, down, CONTRACT_LAST, preferred_element_type=jnp.float32)
        summed = lax.psum(part.astype(jnp.bfloat16), "tensor").astype(jnp.float32)
        out = (wide + summed).astype(jnp.bfloat16)
        final = jnp.where(section == tick, out, final)
        if tick < sections - 1:
            state = lax.ppermute(out, "section", pairs)
    sents = lens.shape[0]
    shaped = final.astype(jnp.float32).reshape(sents, -1, width)
    positions = jnp.arange(shaped.shape[1], dtype=jnp.int32)
    weights = (positions[None, :] < lens[:, None]).astype(jnp.float32)
    pooled = jnp.sum(shaped * weights[:, :, None], axis=1) / lens.astype(jnp.float32)[:, None]
    mean = lax.psum(jnp.sum(pooled, axis=1, keepdims=True), "dp") / d_model
    centered = pooled - mean
    var = lax.psum(jnp.sum(centered * centered, axis=1, keepdims=True), "dp") / d_model
    unit = (centered * lax.rsqrt(var + UNIT_FLOOR)).astype(jnp.bfloat16)
    products = lax.dot_general(unit, unit, CONTRACT_LAST, preferred_element_type=jnp.float32)
    products = lax.psum_scatter(products, "dp", scatter_dimension=0, tiled=True)
    return (1.0 - products / d_model)[None]


def solution(mesh):
    placed = (
        P("dp", "tensor"),
        P("section", None),
        P("section", "dp", "tensor"),
        P("section", "dp", "tensor"),
        P("section", "dp", "tensor"),
        P("dp"),
    )
    return jax.shard_map(
        per_device, mesh=mesh, in_specs=placed, out_specs=P("section", "dp", None), check_vma=False
    )
```

profile of v0, /device:TPU:0, one launch (start us, length us, event | category | flops | bytes accessed | tf_op | source)
XLA Modules:
  0.0 573.4 jit_solution(8479298247538401880)
XLA Ops:
  15.9 9.2 %all-to-all-done = bf16[32,4,1024]{2,0,1:T(8,128)(2,1)S(1)} async-done(((bf16[32,4,1024]{2,0,1:T(8,128)(2,1)}), bf16[32,4,1024]{2,0,1:T(8,128)(2,1)S(1)}, u32[]{:S(2)}, u32[]{:S(2)}) %all-to-all-start) | async-done | bytes 262176 | tf_op jit(solution)/shard_map/all_to_all | solution.py:21
  25.4 9.8 %psum.70 = f32[128,1]{0,1:T(1,128)S(1)} all-reduce(f32[128,1]{0,1:T(1,128)S(1)} %broadcast_in_dim.14), channel_id=1, replica_groups=mesh['section'=4,'tensor'=2,'dp'=4] {'dp'}, use_global_device_ids=true, to_apply=%region_1.0 | all-reduce | flops 128 | bytes 1024 | tf_op jit(solution)/shard_map/psum | solution.py:27
  43.9 42.0 %reduce-scatter.5.cloned.1.call-done = bf16[32,8192]{1,0:T(8,128)(2,1)} async-done(((bf16[128,8192]{1,0:T(8,128)(2,1)}), bf16[32,8192]{1,0:T(8,128)(2,1)}) %reduce-scatter.5.cloned.1.call-update) | async-done | bytes 524304 | tf_op jit(solution)/shard_map/reduce_scatter | solution.py:31
  87.9 27.3 %all-gather.5.cloned.1.call-done = bf16[128,4096]{1,0:T(8,128)(2,1)} async-done(((bf16[32,4096]{1,0:T(8,128)(2,1)}), bf16[128,4096]{1,0:T(8,128)(2,1)}) %all-gather.5.cloned.1.call-update) | async-done | bytes 1048592 | tf_op jit(solution)/shard_map/all_gather | solution.py:37
  115.2 7.3 %fusion.48 = bf16[128,1024]{1,0:T(8,128)(2,1)} fusion(bf16[128,4096]{1,0:T(8,128)(2,1)} %all-gather.5.cloned.1.call-done, bf16[1,1024,4096]{2,1,0:T(8,128)(2,1)} %param.10), kind=kOutput, calls=%fused_computation.36 | convolution fusion | flops 1073872896 | bytes 9699328 | tf_op jit(solution)/shard_map/dot_general | solution.py:38
  122.6 17.7 %all-reduce.7.cloned.1.call-done = bf16[128,1024]{1,0:T(8,128)(2,1)} async-done(((bf16[128,1024]{1,0:T(8,128)(2,1)}), bf16[128,1024]{1,0:T(8,128)(2,1)}) %all-reduce.7.cloned.1.call-update) | async-done | bytes 262160 | tf_op jit(solution)/shard_map/psum | solution.py:39
  151.1 11.7 %psum.72 = f32[128,1]{0,1:T(1,128)S(1)} all-reduce(f32[128,1]{0,1:T(1,128)S(1)} %bitcast.112), channel_id=1, replica_groups=mesh['section'=4,'tensor'=2,'dp'=4] {'dp'}, use_global_device_ids=true, to_apply=%region_5.6 | all-reduce | flops 128 | bytes 1024 | tf_op jit(solution)/shard_map/psum | solution.py:27
  173.8 42.9 %reduce-scatter.7.cloned.1.call-done = bf16[32,8192]{1,0:T(8,128)(2,1)} async-done(((bf16[128,8192]{1,0:T(8,128)(2,1)}), bf16[32,8192]{1,0:T(8,128)(2,1)}) %reduce-scatter.7.cloned.1.call-update) | async-done | bytes 524304 | tf_op jit(solution)/shard_map/reduce_scatter | solution.py:31
  218.8 27.3 %all-gather.7.cloned.1.call-done = bf16[128,4096]{1,0:T(8,128)(2,1)} async-done(((bf16[32,4096]{1,0:T(8,128)(2,1)}), bf16[128,4096]{1,0:T(8,128)(2,1)}) %all-gather.7.cloned.1.call-update) | async-done | bytes 1048592 | tf_op jit(solution)/shard_map/all_gather | solution.py:37
  246.1 7.3 %fusion.51 = bf16[128,1024]{1,0:T(8,128)(2,1)} fusion(bf16[128,4096]{1,0:T(8,128)(2,1)} %all-gather.7.cloned.1.call-done, bf16[1,1024,4096]{2,1,0:T(8,128)(2,1)} %param.10), kind=kOutput, calls=%fused_computation.37 | convolution fusion | flops 1073872896 | bytes 9699328 | tf_op jit(solution)/shard_map/dot_general | solution.py:38
  253.5 17.7 %all-reduce.9.cloned.1.call-done = bf16[128,1024]{1,0:T(8,128)(2,1)} async-done(((bf16[128,1024]{1,0:T(8,128)(2,1)}), bf16[128,1024]{1,0:T(8,128)(2,1)}) %all-reduce.9.cloned.1.call-update) | async-done | bytes 262160 | tf_op jit(solution)/shard_map/psum | solution.py:39
  282.0 11.9 %psum.74 = f32[128,1]{0,1:T(1,128)S(1)} all-reduce(f32[128,1]{0,1:T(1,128)S(1)} %bitcast.113), channel_id=1, replica_groups=mesh['section'=4,'tensor'=2,'dp'=4] {'dp'}, use_global_device_ids=true, to_apply=%region_9.10 | all-reduce | flops 128 | bytes 1024 | tf_op jit(solution)/shard_map/psum | solution.py:27
  304.9 42.9 %reduce-scatter.9.cloned.1.call-done = bf16[32,8192]{1,0:T(8,128)(2,1)} async-done(((bf16[128,8192]{1,0:T(8,128)(2,1)}), bf16[32,8192]{1,0:T(8,128)(2,1)}) %reduce-scatter.9.cloned.1.call-update) | async-done | bytes 524304 | tf_op jit(solution)/shard_map/reduce_scatter | solution.py:31
  349.8 27.3 %all-gather.9.cloned.1.call-done = bf16[128,4096]{1,0:T(8,128)(2,1)} async-done(((bf16[32,4096]{1,0:T(8,128)(2,1)}), bf16[128,4096]{1,0:T(8,128)(2,1)}) %all-gather.9.cloned.1.call-update) | async-done | bytes 1048592 | tf_op jit(solution)/shard_map/all_gather | solution.py:37
  377.1 7.3 %fusion.54 = bf16[128,1024]{1,0:T(8,128)(2,1)} fusion(bf16[128,4096]{1,0:T(8,128)(2,1)} %all-gather.9.cloned.1.call-done, bf16[1,1024,4096]{2,1,0:T(8,128)(2,1)} %param.10), kind=kOutput, calls=%fused_computation.38 | convolution fusion | flops 1073872896 | bytes 9699328 | tf_op jit(solution)/shard_map/dot_general | solution.py:38
  384.5 17.7 %all-reduce.11.cloned.1.call-done = bf16[128,1024]{1,0:T(8,128)(2,1)} async-done(((bf16[128,1024]{1,0:T(8,128)(2,1)}), bf16[128,1024]{1,0:T(8,128)(2,1)}) %all-reduce.11.cloned.1.call-update) | async-done | bytes 262160 | tf_op jit(solution)/shard_map/psum | solution.py:39
  413.1 11.7 %psum.76 = f32[128,1]{0,1:T(1,128)S(1)} all-reduce(f32[128,1]{0,1:T(1,128)S(1)} %bitcast.114), channel_id=1, replica_groups=mesh['section'=4,'tensor'=2,'dp'=4] {'dp'}, use_global_device_ids=true, to_apply=%region_13.14 | all-reduce | flops 128 | bytes 1024 | tf_op jit(solution)/shard_map/psum | solution.py:27
  435.8 42.9 %reduce-scatter.11.cloned.1.call-done = bf16[32,8192]{1,0:T(8,128)(2,1)} async-done(((bf16[128,8192]{1,0:T(8,128)(2,1)}), bf16[32,8192]{1,0:T(8,128)(2,1)}) %reduce-scatter.11.cloned.1.call-update) | async-done | bytes 524304 | tf_op jit(solution)/shard_map/reduce_scatter | solution.py:31
  480.7 27.3 %all-gather.11.cloned.1.call-done = bf16[128,4096]{1,0:T(8,128)(2,1)} async-done(((bf16[32,4096]{1,0:T(8,128)(2,1)}), bf16[128,4096]{1,0:T(8,128)(2,1)}) %all-gather.11.cloned.1.call-update) | async-done | bytes 1048592 | tf_op jit(solution)/shard_map/all_gather | solution.py:37
  517.0 7.7 %all-reduce = s32[16]{0:T(128)S(1)} all-reduce(s32[16]{0:T(128)S(1)} %dynamic-update-slice), channel_id=1, replica_groups=mesh['section'=4,'tensor'=2,'dp'=4] {'dp'}, use_global_device_ids=true, to_apply=%add | all-reduce | flops 16 | bytes 128
  525.4 7.8 %all-reduce.13.cloned.1.call-done = bf16[128,1024]{1,0:T(8,128)(2,1)} async-done(((bf16[128,1024]{1,0:T(8,128)(2,1)}), bf16[128,1024]{1,0:T(8,128)(2,1)}) %all-reduce.13.cloned.1.call-update) | async-done | bytes 262160 | tf_op jit(solution)/shard_map/psum | solution.py:39
  534.7 12.0 %psum.78 = f32[16,1]{0,1:T(1,128)S(1)} all-reduce(f32[16,1]{0,1:T(1,128)S(1)} %bitcast.115), channel_id=1, replica_groups=mesh['section'=4,'tensor'=2,'dp'=4] {'dp'}, use_global_device_ids=true, to_apply=%region_18.19 | all-reduce | flops 16 | bytes 128 | tf_op jit(solution)/shard_map/psum | solution.py:49
  546.9 8.4 %psum.79 = f32[16,1]{0,1:T(1,128)S(1)} all-reduce(f32[16,1]{0,1:T(1,128)S(1)} %bitcast.116), channel_id=1, replica_groups=mesh['section'=4,'tensor'=2,'dp'=4] {'dp'}, use_global_device_ids=true, to_apply=%region_20.21 | all-reduce | flops 16 | bytes 128 | tf_op jit(solution)/shard_map/psum | solution.py:51
  555.5 10.5 %all-reduce.1 = f32[16,16]{1,0:T(8,128)S(1)} all-reduce(f32[16,16]{1,0:T(8,128)S(1)} %fusion.90), channel_id=6, replica_groups=mesh['section'=4,'tensor'=2,'dp'=4] {'dp'}, use_global_device_ids=true, to_apply=%region_21.22.clone | all-reduce | flops 256 | bytes 2048
  (91 shorter events, 102.9 us)
Async XLA Ops:
  6.5 9.4 %copy-start = (f32[1,4096]{1,0:T(1,128)S(1)}, f32[1,4096]{1,0:T(1,128)}, u32[]{:S(2)}) copy-start(f32[1,4096]{1,0:T(1,128)} %param.7) | copy-start | bytes 49156
  9.7 15.4 %all-to-all-start = ((bf16[32,4,1024]{2,0,1:T(8,128)(2,1)}), bf16[32,4,1024]{2,0,1:T(8,128)(2,1)S(1)}, u32[]{:S(2)}, u32[]{:S(2)}) async-start(bf16[32,4,1024]{2,0,1:T(8,128)(2,1)} %bitcast.101), calls=%async_computation | async-start | bytes 524288 | tf_op jit(solution)/shard_map/all_to_all | solution.py:21
  15.9 69.9 %reduce-scatter.5.cloned.1.call-start = ((), (), s32[]{:S(2)}) async-start(), calls=%async_computation.5 | async-start | bytes 2621440 | tf_op jit(solution)/shard_map/reduce_scatter | solution.py:31
  35.2 5.8 %copy-start.1 = (bf16[1,1024,4096]{2,1,0:T(8,128)(2,1)S(1)}, bf16[1,1024,4096]{2,1,0:T(8,128)(2,1)}, u32[]{:S(2)}) copy-start(bf16[1,1024,4096]{2,1,0:T(8,128)(2,1)} %param.9) | copy-start | bytes 25165828
  43.8 71.4 %all-gather.5.cloned.1.call-start = ((), (), s32[]{:S(2)}) async-start(), calls=%async_computation.6 | async-start | bytes 1310720 | tf_op jit(solution)/shard_map/all_gather | solution.py:37
  87.8 52.5 %all-reduce.7.cloned.1.call-start = ((), (), s32[]{:S(2)}) async-start(), calls=%async_computation.7 | async-start | bytes 524288 | tf_op jit(solution)/shard_map/psum | solution.py:39
  122.5 94.2 %reduce-scatter.7.cloned.1.call-start = ((), (), s32[]{:S(2)}) async-start(), calls=%async_computation.8 | async-start | bytes 2621440 | tf_op jit(solution)/shard_map/reduce_scatter | solution.py:31
  141.3 9.7 %collective-permute-start = (bf16[128,1024]{1,0:T(8,128)(2,1)S(1)}, bf16[128,1024]{1,0:T(8,128)(2,1)S(1)}, u32[]{:S(2)}, u32[]{:S(2)}) collective-permute-start(bf16[128,1024]{1,0:T(8,128)(2,1)S(1)} %add_convert_fusion), channel_id=1, source_target_pairs={{0,8},{8,16},{16,24},{1,9},{9,17},{17,25},{2,10},{10,18},{18,26},{... | collective-permute-start | bytes 786440 | tf_op jit(solution)/shard_map/ppermute | solution.py:43
  173.8 72.3 %all-gather.7.cloned.1.call-start = ((), (), s32[]{:S(2)}) async-start(), calls=%async_computation.9 | async-start | bytes 1310720 | tf_op jit(solution)/shard_map/all_gather | solution.py:37
  218.7 52.4 %all-reduce.9.cloned.1.call-start = ((), (), s32[]{:S(2)}) async-start(), calls=%async_computation.10 | async-start | bytes 524288 | tf_op jit(solution)/shard_map/psum | solution.py:39
  253.4 94.4 %reduce-scatter.9.cloned.1.call-start = ((), (), s32[]{:S(2)}) async-start(), calls=%async_computation.11 | async-start | bytes 2621440 | tf_op jit(solution)/shard_map/reduce_scatter | solution.py:31
  272.2 9.7 %collective-permute-start.1 = (bf16[128,1024]{1,0:T(8,128)(2,1)S(1)}, bf16[128,1024]{1,0:T(8,128)(2,1)S(1)}, u32[]{:S(2)}, u32[]{:S(2)}) collective-permute-start(bf16[128,1024]{1,0:T(8,128)(2,1)S(1)} %fusion.66), channel_id=1, source_target_pairs={{0,8},{8,16},{16,24},{1,9},{9,17},{17,25},{2,10},{10,18},{18,26},{... | collective-permute-start | bytes 786440 | tf_op jit(solution)/shard_map/ppermute | solution.py:43
  304.8 72.3 %all-gather.9.cloned.1.call-start = ((), (), s32[]{:S(2)}) async-start(), calls=%async_computation.12 | async-start | bytes 1310720 | tf_op jit(solution)/shard_map/all_gather | solution.py:37
  349.8 52.4 %all-reduce.11.cloned.1.call-start = ((), (), s32[]{:S(2)}) async-start(), calls=%async_computation.13 | async-start | bytes 524288 | tf_op jit(solution)/shard_map/psum | solution.py:39
  384.5 94.2 %reduce-scatter.11.cloned.1.call-start = ((), (), s32[]{:S(2)}) async-start(), calls=%async_computation.14 | async-start | bytes 2621440 | tf_op jit(solution)/shard_map/reduce_scatter | solution.py:31
  403.3 9.7 %collective-permute-start.2 = (bf16[128,1024]{1,0:T(8,128)(2,1)S(1)}, bf16[128,1024]{1,0:T(8,128)(2,1)S(1)}, u32[]{:S(2)}, u32[]{:S(2)}) collective-permute-start(bf16[128,1024]{1,0:T(8,128)(2,1)S(1)} %fusion.70), channel_id=1, source_target_pairs={{0,8},{8,16},{16,24},{1,9},{9,17},{17,25},{2,10},{10,18},{18,26},{... | collective-permute-start | bytes 786440 | tf_op jit(solution)/shard_map/ppermute | solution.py:43
  435.7 79.7 %copy-start.3 = (u32[32]{0:T(128)S(1)}, u32[32]{0:T(128)}, u32[]{:S(2)}) copy-start(u32[32]{0:T(128)} %constant.50) | copy-start | bytes 388
  435.7 81.0 %copy-start.4 = (s32[4]{0:T(128)S(1)}, s32[4]{0:T(128)}, u32[]{:S(2)}) copy-start(s32[4]{0:T(128)} %param.11) | copy-start | bytes 52
  435.7 97.4 %copy-start.2 = (bf16[128,1024]{1,0:T(8,128)(2,1)S(1)}, bf16[128,1024]{1,0:T(8,128)(2,1)}, u32[]{:S(2)}) copy-start(bf16[128,1024]{1,0:T(8,128)(2,1)} %all-reduce.7.cloned.1.call-done) | copy-start | bytes 786436
  435.7 72.3 %all-gather.11.cloned.1.call-start = ((), (), s32[]{:S(2)}) async-start(), calls=%async_computation.15 | async-start | bytes 1310720 | tf_op jit(solution)/shard_map/all_gather | solution.py:37
  480.7 52.4 %all-reduce.13.cloned.1.call-start = ((), (), s32[]{:S(2)}) async-start(), calls=%async_computation.16 | async-start | bytes 524288 | tf_op jit(solution)/shard_map/psum | solution.py:39
Sparse Core Ops, SparseCore 0:
  43.9 41.8 reduce-scatter.4
  88.0 27.1 all-gather.4
  122.7 17.5 all-reduce.6
  173.9 42.7 reduce-scatter.6
  218.8 27.1 all-gather.6
  253.5 17.5 all-reduce.8
  305.0 42.7 reduce-scatter.8
  349.9 27.1 all-gather.8
  384.6 17.5 all-reduce.10
  435.9 42.7 reduce-scatter.10
  480.8 27.1 all-gather.10
  515.5 17.5 all-reduce.12
where the time goes:
time: 574 us; the launch traced here: 573 us
  waiting for transfers between devices  368 us (64%)
  blocking collectives  86 us (15%)
  matrix products  63.9 us (11%)
  other arithmetic  20.2 us (4%)
  starting transfers between devices  17.8 us (3%)
  between operations  15.1 us (3%)
    reduce_scatter x4, waiting for transfers between devices, per_device(): lax.psum_scatter(jnp.concatenate([g, u], axis=1), 'dp', scatter_dimension...  171 us
    all_gather x4, waiting for transfers between devices, per_device(): hidden = lax.all_gather(hidden, 'dp', axis=0, tiled=True)  109 us
    psum x4, waiting for transfers between devices, per_device(): summed = lax.psum(part.astype(jnp.bfloat16), 'tensor').astype(jnp.float32)  60.9 us
    psum x4, blocking collectives, per_device(): total = lax.psum(jnp.sum(wide * wide, axis=1, keepdims=True), 'dp')  45 us
    dot_general x4, matrix products, per_device(): lax.dot_general(hidden, down, CONTRACT_LAST, preferred_element_type=jnp.f...  29.4 us
    dot_general x4, matrix products, per_device(): jnp.dot(normed, gate, preferred_element_type=jnp.float32)  18.9 us
    unnamed x2, blocking collectives  18.2 us
    ppermute x3, waiting for transfers between devices, per_device(): state = lax.ppermute(out, 'section', pairs)  17.9 us
  transfers between devices with their start and end apart: 16, of which 16 were waited for; matrix products, arithmetic and copies ran while one was open for 0% of the time, Pallas kernels for 0%

commit v1 on v0

--- a/solution.py
+++ b/solution.py
@@ -36,7 +36,9 @@
         hidden = (jax.nn.silu(both[:, :cols]) * both[:, cols:]).astype(jnp.bfloat16)
         hidden = lax.all_gather(hidden, "dp", axis=0, tiled=True)
         part = lax.dot_general(hidden, down, CONTRACT_LAST, preferred_element_type=jnp.float32)
-        summed = lax.psum(part.astype(jnp.bfloat16), "tensor").astype(jnp.float32)
+        summed = jnp.sum(lax.all_gather(part.astype(jnp.bfloat16), "tensor"), axis=0).astype(
+            jnp.float32
+        )
         out = (wide + summed).astype(jnp.bfloat16)
         final = jnp.where(section == tick, out, final)
         if tick < sections - 1:

time: 574 us -> 498 us (0.87)
  waiting for transfers between devices: 368 us -> 297 us
    psum x4 -> x0, waiting for transfers between devices: 60.9 us -> none  [per_device(): summed = lax.psum(part.astype(jnp.bfloat16), 'tensor').astype(jnp.float32)]
    all_gather x4, waiting for transfers between devices: 109 us -> 99.5 us  [per_device(): hidden = lax.all_gather(hidden, 'dp', axis=0, tiled=True)]
    all_gather x0 -> x4, blocking collectives: none -> 8.73 us  [per_device(): lax.all_gather(part.astype(jnp.bfloat16), 'tensor')]
  transfers between devices with their start and end apart: 16 -> 12, of which waited for: 16 -> 12; matrix products, arithmetic and copies ran while one was open for 0% -> 0% of each run, Pallas kernels for 0% -> 0%
where the time goes in v1:
time: 498 us; the launch traced here: 497 us
  waiting for transfers between devices  297 us (60%)
  blocking collectives  88.1 us (18%)
  matrix products  61 us (12%)
  other arithmetic  16.8 us (3%)
  starting transfers between devices  16.7 us (3%)
  between operations  15.1 us (3%)
    reduce_scatter x4, waiting for transfers between devices, per_device(): lax.psum_scatter(jnp.concatenate([g, u], axis=1), 'dp', scatter_dimension...  171 us
    all_gather x4, waiting for transfers between devices, per_device(): hidden = lax.all_gather(hidden, 'dp', axis=0, tiled=True)  99.5 us
    psum x4, blocking collectives, per_device(): total = lax.psum(jnp.sum(wide * wide, axis=1, keepdims=True), 'dp')  40.4 us
    dot_general x4, matrix products, per_device(): lax.dot_general(hidden, down, CONTRACT_LAST, preferred_element_type=jnp.f...  26.5 us
    dot_general x4, matrix products, per_device(): jnp.dot(normed, gate, preferred_element_type=jnp.float32)  18.9 us
    unnamed x2, blocking collectives  17.7 us
    ppermute x3, waiting for transfers between devices, per_device(): state = lax.ppermute(out, 'section', pairs)  17.5 us
    dot_general x4, matrix products, per_device(): jnp.dot(normed, up, preferred_element_type=jnp.float32).astype(jnp.bfloat16)  15.4 us
  transfers between devices with their start and end apart: 12, of which 12 were waited for; matrix products, arithmetic and copies ran while one was open for 0% of the time, Pallas kernels for 0%

profile of v1, /device:TPU:0, one launch (start us, length us, event | category | flops | bytes accessed | tf_op | source)
XLA Modules:
  0.0 497.1 jit_solution(12644474278995464507)
XLA Ops:
  9.7 6.2 %all-to-all-start = ((bf16[32,4,1024]{2,0,1:T(8,128)(2,1)}), bf16[32,4,1024]{2,0,1:T(8,128)(2,1)S(1)}, u32[]{:S(2)}, u32[]{:S(2)}) async-start(bf16[32,4,1024]{2,0,1:T(8,128)(2,1)} %bitcast.105), calls=%async_computation | async-start | bytes 524288 | tf_op jit(solution)/shard_map/all_to_all | solution.py:21
  15.9 9.2 %all-to-all-done = bf16[32,4,1024]{2,0,1:T(8,128)(2,1)S(1)} async-done(((bf16[32,4,1024]{2,0,1:T(8,128)(2,1)}), bf16[32,4,1024]{2,0,1:T(8,128)(2,1)S(1)}, u32[]{:S(2)}, u32[]{:S(2)}) %all-to-all-start) | async-done | bytes 262176 | tf_op jit(solution)/shard_map/all_to_all | solution.py:21
  25.4 9.8 %psum.42 = f32[128,1]{0,1:T(1,128)S(1)} all-reduce(f32[128,1]{0,1:T(1,128)S(1)} %broadcast_in_dim.14), channel_id=1, replica_groups=mesh['section'=4,'tensor'=2,'dp'=4] {'dp'}, use_global_device_ids=true, to_apply=%region_1.0 | all-reduce | flops 128 | bytes 1024 | tf_op jit(solution)/shard_map/psum | solution.py:27
  43.9 42.0 %reduce-scatter.5.cloned.1.call-done = bf16[32,8192]{1,0:T(8,128)(2,1)} async-done(((bf16[128,8192]{1,0:T(8,128)(2,1)}), bf16[32,8192]{1,0:T(8,128)(2,1)}) %reduce-scatter.5.cloned.1.call-update) | async-done | bytes 524304 | tf_op jit(solution)/shard_map/reduce_scatter | solution.py:31
  87.9 27.3 %all-gather.9.cloned.1.call-done = bf16[128,4096]{1,0:T(8,128)(2,1)} async-done(((bf16[32,4096]{1,0:T(8,128)(2,1)}), bf16[128,4096]{1,0:T(8,128)(2,1)}) %all-gather.9.cloned.1.call-update) | async-done | bytes 1048592 | tf_op jit(solution)/shard_map/all_gather | solution.py:37
  115.2 6.6 %fusion.48 = bf16[128,1024]{1,0:T(8,128)(2,1)S(1)} fusion(bf16[128,4096]{1,0:T(8,128)(2,1)} %all-gather.9.cloned.1.call-done, bf16[1,1024,4096]{2,1,0:T(8,128)(2,1)} %param.10), kind=kOutput, calls=%fused_computation.36 | convolution fusion | flops 1073872896 | bytes 9699328 | tf_op jit(solution)/shard_map/dot_general | solution.py:38
  127.6 5.8 %collective-permute-done = bf16[128,1024]{1,0:T(8,128)(2,1)S(1)} collective-permute-done((bf16[128,1024]{1,0:T(8,128)(2,1)S(1)}, bf16[128,1024]{1,0:T(8,128)(2,1)S(1)}, u32[]{:S(2)}, u32[]{:S(2)}) %collective-permute-start) | collective-permute-done | bytes 262176 | tf_op jit(solution)/shard_map/ppermute | solution.py:45
  133.5 10.2 %psum.43 = f32[128,1]{0,1:T(1,128)S(1)} all-reduce(f32[128,1]{0,1:T(1,128)S(1)} %bitcast.120), channel_id=1, replica_groups=mesh['section'=4,'tensor'=2,'dp'=4] {'dp'}, use_global_device_ids=true, to_apply=%region_5.6 | all-reduce | flops 128 | bytes 1024 | tf_op jit(solution)/shard_map/psum | solution.py:27
  154.7 42.9 %reduce-scatter.7.cloned.1.call-done = bf16[32,8192]{1,0:T(8,128)(2,1)} async-done(((bf16[128,8192]{1,0:T(8,128)(2,1)}), bf16[32,8192]{1,0:T(8,128)(2,1)}) %reduce-scatter.7.cloned.1.call-update) | async-done | bytes 524304 | tf_op jit(solution)/shard_map/reduce_scatter | solution.py:31
  199.7 27.3 %all-gather.11.cloned.1.call-done = bf16[128,4096]{1,0:T(8,128)(2,1)} async-done(((bf16[32,4096]{1,0:T(8,128)(2,1)}), bf16[128,4096]{1,0:T(8,128)(2,1)}) %all-gather.11.cloned.1.call-update) | async-done | bytes 1048592 | tf_op jit(solution)/shard_map/all_gather | solution.py:37
  227.0 6.6 %fusion.51 = bf16[128,1024]{1,0:T(8,128)(2,1)S(1)} fusion(bf16[128,4096]{1,0:T(8,128)(2,1)} %all-gather.11.cloned.1.call-done, bf16[1,1024,4096]{2,1,0:T(8,128)(2,1)} %param.10), kind=kOutput, calls=%fused_computation.37 | convolution fusion | flops 1073872896 | bytes 9699328 | tf_op jit(solution)/shard_map/dot_general | solution.py:38
  239.3 5.8 %collective-permute-done.1 = bf16[128,1024]{1,0:T(8,128)(2,1)S(1)} collective-permute-done((bf16[128,1024]{1,0:T(8,128)(2,1)S(1)}, bf16[128,1024]{1,0:T(8,128)(2,1)S(1)}, u32[]{:S(2)}, u32[]{:S(2)}) %collective-permute-start.1) | collective-permute-done | bytes 262176 | tf_op jit(solution)/shard_map/ppermute | solution.py:45
  245.3 10.3 %psum.44 = f32[128,1]{0,1:T(1,128)S(1)} all-reduce(f32[128,1]{0,1:T(1,128)S(1)} %bitcast.121), channel_id=1, replica_groups=mesh['section'=4,'tensor'=2,'dp'=4] {'dp'}, use_global_device_ids=true, to_apply=%region_9.10 | all-reduce | flops 128 | bytes 1024 | tf_op jit(solution)/shard_map/psum | solution.py:27
  266.7 42.9 %reduce-scatter.9.cloned.1.call-done = bf16[32,8192]{1,0:T(8,128)(2,1)} async-done(((bf16[128,8192]{1,0:T(8,128)(2,1)}), bf16[32,8192]{1,0:T(8,128)(2,1)}) %reduce-scatter.9.cloned.1.call-update) | async-done | bytes 524304 | tf_op jit(solution)/shard_map/reduce_scatter | solution.py:31
  311.6 27.3 %all-gather.13.cloned.1.call-done = bf16[128,4096]{1,0:T(8,128)(2,1)} async-done(((bf16[32,4096]{1,0:T(8,128)(2,1)}), bf16[128,4096]{1,0:T(8,128)(2,1)}) %all-gather.13.cloned.1.call-update) | async-done | bytes 1048592 | tf_op jit(solution)/shard_map/all_gather | solution.py:37
  338.9 6.6 %fusion.54 = bf16[128,1024]{1,0:T(8,128)(2,1)S(1)} fusion(bf16[128,4096]{1,0:T(8,128)(2,1)} %all-gather.13.cloned.1.call-done, bf16[1,1024,4096]{2,1,0:T(8,128)(2,1)} %param.10), kind=kOutput, calls=%fused_computation.38 | convolution fusion | flops 1073872896 | bytes 9699328 | tf_op jit(solution)/shard_map/dot_general | solution.py:38
  357.2 10.2 %psum.45 = f32[128,1]{0,1:T(1,128)S(1)} all-reduce(f32[128,1]{0,1:T(1,128)S(1)} %bitcast.122), channel_id=1, replica_groups=mesh['section'=4,'tensor'=2,'dp'=4] {'dp'}, use_global_device_ids=true, to_apply=%region_13.14 | all-reduce | flops 128 | bytes 1024 | tf_op jit(solution)/shard_map/psum | solution.py:27
  378.4 42.9 %reduce-scatter.11.cloned.1.call-done = bf16[32,8192]{1,0:T(8,128)(2,1)} async-done(((bf16[128,8192]{1,0:T(8,128)(2,1)}), bf16[32,8192]{1,0:T(8,128)(2,1)}) %reduce-scatter.11.cloned.1.call-update) | async-done | bytes 524304 | tf_op jit(solution)/shard_map/reduce_scatter | solution.py:31
  424.9 7.5 %all-reduce = s32[16]{0:T(128)S(1)} all-reduce(s32[16]{0:T(128)S(1)} %dynamic-update-slice), channel_id=1, replica_groups=mesh['section'=4,'tensor'=2,'dp'=4] {'dp'}, use_global_device_ids=true, to_apply=%add | all-reduce | flops 16 | bytes 128
  433.1 17.6 %all-gather.15.cloned.1.call-done = bf16[128,4096]{1,0:T(8,128)(2,1)} async-done(((bf16[32,4096]{1,0:T(8,128)(2,1)}), bf16[128,4096]{1,0:T(8,128)(2,1)}) %all-gather.15.cloned.1.call-update) | async-done | bytes 1048592 | tf_op jit(solution)/shard_map/all_gather | solution.py:37
  450.7 6.6 %fusion.57 = bf16[128,1024]{1,0:T(8,128)(2,1)S(1)} fusion(bf16[128,4096]{1,0:T(8,128)(2,1)} %all-gather.15.cloned.1.call-done, bf16[1,1024,4096]{2,1,0:T(8,128)(2,1)} %param.10), kind=kOutput, calls=%fused_computation.39 | convolution fusion | flops 1073872896 | bytes 9699328 | tf_op jit(solution)/shard_map/dot_general | solution.py:38
  460.3 10.1 %psum.46 = f32[16,1]{0,1:T(1,128)S(1)} all-reduce(f32[16,1]{0,1:T(1,128)S(1)} %bitcast.123), channel_id=1, replica_groups=mesh['section'=4,'tensor'=2,'dp'=4] {'dp'}, use_global_device_ids=true, to_apply=%region_18.19 | all-reduce | flops 16 | bytes 128 | tf_op jit(solution)/shard_map/psum | solution.py:51
  470.6 8.6 %psum.47 = f32[16,1]{0,1:T(1,128)S(1)} all-reduce(f32[16,1]{0,1:T(1,128)S(1)} %bitcast.124), channel_id=1, replica_groups=mesh['section'=4,'tensor'=2,'dp'=4] {'dp'}, use_global_device_ids=true, to_apply=%region_20.21 | all-reduce | flops 16 | bytes 128 | tf_op jit(solution)/shard_map/psum | solution.py:53
  479.4 10.3 %all-reduce.1 = f32[16,16]{1,0:T(8,128)S(1)} all-reduce(f32[16,16]{1,0:T(8,128)S(1)} %fusion.90), channel_id=10, replica_groups=mesh['section'=4,'tensor'=2,'dp'=4] {'dp'}, use_global_device_ids=true, to_apply=%region_21.22.clone | all-reduce | flops 256 | bytes 2048
  (85 shorter events, 81.5 us)
Async XLA Ops:
  6.5 9.4 %copy-start = (f32[1,4096]{1,0:T(1,128)S(1)}, f32[1,4096]{1,0:T(1,128)}, u32[]{:S(2)}) copy-start(f32[1,4096]{1,0:T(1,128)} %param.7) | copy-start | bytes 49156
  9.7 15.4 %all-to-all-start = ((bf16[32,4,1024]{2,0,1:T(8,128)(2,1)}), bf16[32,4,1024]{2,0,1:T(8,128)(2,1)S(1)}, u32[]{:S(2)}, u32[]{:S(2)}) async-start(bf16[32,4,1024]{2,0,1:T(8,128)(2,1)} %bitcast.105), calls=%async_computation | async-start | bytes 524288 | tf_op jit(solution)/shard_map/all_to_all | solution.py:21
  15.9 69.9 %reduce-scatter.5.cloned.1.call-start = ((), (), s32[]{:S(2)}) async-start(), calls=%async_computation.5 | async-start | bytes 2621440 | tf_op jit(solution)/shard_map/reduce_scatter | solution.py:31
  35.2 5.8 %copy-start.1 = (bf16[1,1024,4096]{2,1,0:T(8,128)(2,1)S(1)}, bf16[1,1024,4096]{2,1,0:T(8,128)(2,1)}, u32[]{:S(2)}) copy-start(bf16[1,1024,4096]{2,1,0:T(8,128)(2,1)} %param.9) | copy-start | bytes 25165828
  43.8 71.4 %all-gather.9.cloned.1.call-start = ((), (), s32[]{:S(2)}) async-start(), calls=%async_computation.6 | async-start | bytes 1310720 | tf_op jit(solution)/shard_map/all_gather | solution.py:37
  87.9 109.8 %reduce-scatter.7.cloned.1.call-start = ((), (), s32[]{:S(2)}) async-start(), calls=%async_computation.7 | async-start | bytes 2621440 | tf_op jit(solution)/shard_map/reduce_scatter | solution.py:31
  124.2 9.2 %collective-permute-start = (bf16[128,1024]{1,0:T(8,128)(2,1)S(1)}, bf16[128,1024]{1,0:T(8,128)(2,1)S(1)}, u32[]{:S(2)}, u32[]{:S(2)}) collective-permute-start(bf16[128,1024]{1,0:T(8,128)(2,1)S(1)} %add_convert_fusion), channel_id=1, source_target_pairs={{0,8},{8,16},{16,24},{1,9},{9,17},{17,25},{2,10},{10,18},{18,26},{... | collective-permute-start | bytes 786440 | tf_op jit(solution)/shard_map/ppermute | solution.py:45
  154.7 72.3 %all-gather.11.cloned.1.call-start = ((), (), s32[]{:S(2)}) async-start(), calls=%async_computation.8 | async-start | bytes 1310720 | tf_op jit(solution)/shard_map/all_gather | solution.py:37
  199.6 109.9 %reduce-scatter.9.cloned.1.call-start = ((), (), s32[]{:S(2)}) async-start(), calls=%async_computation.9 | async-start | bytes 2621440 | tf_op jit(solution)/shard_map/reduce_scatter | solution.py:31
  235.9 9.2 %collective-permute-start.1 = (bf16[128,1024]{1,0:T(8,128)(2,1)S(1)}, bf16[128,1024]{1,0:T(8,128)(2,1)S(1)}, u32[]{:S(2)}, u32[]{:S(2)}) collective-permute-start(bf16[128,1024]{1,0:T(8,128)(2,1)S(1)} %fusion.66), channel_id=1, source_target_pairs={{0,8},{8,16},{16,24},{1,9},{9,17},{17,25},{2,10},{10,18},{18,26},{... | collective-permute-start | bytes 786440 | tf_op jit(solution)/shard_map/ppermute | solution.py:45
  266.6 72.3 %all-gather.13.cloned.1.call-start = ((), (), s32[]{:S(2)}) async-start(), calls=%async_computation.10 | async-start | bytes 1310720 | tf_op jit(solution)/shard_map/all_gather | solution.py:37
  311.6 109.8 %reduce-scatter.11.cloned.1.call-start = ((), (), s32[]{:S(2)}) async-start(), calls=%async_computation.11 | async-start | bytes 2621440 | tf_op jit(solution)/shard_map/reduce_scatter | solution.py:31
  347.9 9.2 %collective-permute-start.2 = (bf16[128,1024]{1,0:T(8,128)(2,1)S(1)}, bf16[128,1024]{1,0:T(8,128)(2,1)S(1)}, u32[]{:S(2)}, u32[]{:S(2)}) collective-permute-start(bf16[128,1024]{1,0:T(8,128)(2,1)S(1)} %fusion.70), channel_id=1, source_target_pairs={{0,8},{8,16},{16,24},{1,9},{9,17},{17,25},{2,10},{10,18},{18,26},{... | collective-permute-start | bytes 786440 | tf_op jit(solution)/shard_map/ppermute | solution.py:45
  372.1 51.2 %copy-start.2 = (u32[32]{0:T(128)S(1)}, u32[32]{0:T(128)}, u32[]{:S(2)}) copy-start(u32[32]{0:T(128)} %constant.55) | copy-start | bytes 388
  372.1 52.5 %copy-start.3 = (s32[4]{0:T(128)S(1)}, s32[4]{0:T(128)}, u32[]{:S(2)}) copy-start(s32[4]{0:T(128)} %param.11) | copy-start | bytes 52
  378.4 72.3 %all-gather.15.cloned.1.call-start = ((), (), s32[]{:S(2)}) async-start(), calls=%async_computation.12 | async-start | bytes 1310720 | tf_op jit(solution)/shard_map/all_gather | solution.py:37
Sparse Core Ops, SparseCore 0:
  43.9 41.8 reduce-scatter.4
  88.0 27.1 all-gather.8
  154.8 42.7 reduce-scatter.6
  199.7 27.1 all-gather.10
  266.7 42.7 reduce-scatter.8
  311.7 27.1 all-gather.12
  378.5 42.7 reduce-scatter.10
  423.5 27.2 all-gather.14
